TPU v7x, 32 devices: a whole 2x2x4 slice. The times are simulated.
32 devices in a mesh: row: 8 (over z, core), col: 4 (over y, x).
Axes of the slice: x: 2, y: 2, z: 4, core: 2. Of those that a mesh axis runs over, the one named last changes fastest.
Arguments:
- ancestor_inverse: float32 [12288, 12288], P('row', 'col'), may hold values from -6 to 6
- panel: float32 [5632, 512], P('col', 'row'), may hold values from -0.078125 to 0.078125
- unit_inverse: float32 [512, 512], P('row'), may hold values from -1 to 1, as said below
- pivot_inverse: float32 [512, 512], P('row', 'col'), may hold values from -6 to 6
- panel_blocks: int32 [44], replicated, may hold values from 0 to 95, as said below
Outputs:
- inverse_row: float32 [512, 12288], P('col', 'row')
- diagonal_block: float32 [512, 512], P('row', 'col')
Inputs may be any that keep to these rules, and one draw needn't show every extreme that they name: `panel_blocks`: Distinct, in no particular order. Among the window blocks c * 24 to c * 24 + 23 of any process column c at most 12 are listed, and exactly 12 for some columns. `unit_inverse`: unit lower triangular: ones on the diagonal, zeros above it.
All inputs are finite; a program needn't handle non-finite values.
Results may differ from a plain program's by a relative error of at most 0.00011.
Values sent between devices are 32-bit elements; how exact they have to be, the bound alone decides.
A program may use at most 128 MiB of HBM per device.

v0:
```python
import jax
import jax.numpy as jnp
from jax import lax
from jax.sharding import PartitionSpec as P

BLK = 128


def broadcast(value, axis, root):
    mine = lax.axis_index(axis) == root
    return lax.psum(jnp.where(mine, value, jnp.zeros_like(value)), axis)


def place_blocks(stacked, block_ids, wanted):
    onehot = (block_ids[None, :] == wanted[:, None]).astype(jnp.float32)
    placed = jnp.einsum("kp,pbw->kbw", onehot, stacked, precision=lax.Precision.HIGHEST)
    return placed.reshape(wanted.shape[0] * stacked.shape[1], stacked.shape[2])


def on_device(ancestor_inverse, panel, unit_inverse, pivot_inverse, panel_blocks):
    highest = lax.Precision.HIGHEST
    row_index = lax.axis_index("row")
    col_index = lax.axis_index("col")
    rows_here, cols_here = ancestor_inverse.shape
    width = unit_inverse.shape[1]
    block_total = panel_blocks.shape[0]
    range_blocks = cols_here // BLK
    row_blocks = rows_here // BLK
    first_block = col_index * range_blocks
    partial_value = jnp.dot(
        panel, unit_inverse, precision=highest, preferred_element_type=jnp.float32
    )
    normal = lax.psum_scatter(partial_value, "row", scatter_dimension=1, tiled=True)
    all_rows = lax.all_gather(normal, "col", axis=0, tiled=True)
    stacked = all_rows.reshape(block_total, BLK, all_rows.shape[1])
    slot_count = range_blocks // 2
    in_range = ((panel_blocks >= first_block) & (panel_blocks < first_block + range_blocks)).astype(
        jnp.int32
    )
    rank_of = jnp.cumsum(in_range) - 1
    slot_ids = jnp.arange(slot_count, dtype=jnp.int32)
    selected = (in_range[None, :] == 1) & (rank_of[None, :] == slot_ids[:, None])
    chosen = jnp.einsum("sp,pbw->sbw", selected.astype(jnp.float32), stacked, precision=highest)
    chosen = chosen.reshape(slot_count * BLK, stacked.shape[2])
    chosen_ids = jnp.sum(jnp.where(selected, panel_blocks[None, :], 0), axis=1)
    slot_live = jnp.sum(selected.astype(jnp.int32), axis=1) > 0
    window_ids = jnp.where(slot_live, chosen_ids, -1)
    local_ids = jnp.clip(chosen_ids - first_block, 0, range_blocks - 1)
    window = lax.all_gather(chosen, "row", axis=1, tiled=True)
    columns = jnp.take(ancestor_inverse.reshape(rows_here, range_blocks, BLK), local_ids, axis=1)
    columns = columns.reshape(rows_here, slot_count * BLK)
    inverse_tile = lax.psum_scatter(
        -lax.dot_general(
            window,
            columns,
            (((0,), (1,)), ((), ())),
            precision=highest,
            preferred_element_type=jnp.float32,
        ),
        "col",
        scatter_dimension=0,
        tiled=True,
    )
    row_ids = row_index * row_blocks + jnp.arange(row_blocks, dtype=jnp.int32)
    window_stack = window.reshape(window.shape[0] // BLK, BLK, width)
    candidate = place_blocks(window_stack, window_ids, row_ids)
    owner = row_index * rows_here // cols_here
    own_window = broadcast(candidate, "col", owner)
    crossed = -lax.dot_general(
        own_window,
        inverse_tile,
        (((0,), (1,)), ((), ())),
        precision=highest,
        preferred_element_type=jnp.float32,
    )
    diagonal_block = pivot_inverse + lax.psum_scatter(
        crossed, "row", scatter_dimension=0, tiled=True
    )
    return (inverse_tile, diagonal_block)


def solution(mesh):
    return jax.shard_map(
        on_device,
        mesh=mesh,
        in_specs=(P("row", "col"), P("col", "row"), P("row", None), P("row", "col"), P()),
        out_specs=(P("col", "row"), P("row", "col")),
        check_vma=False,
    )
```

profile of v0, /device:TPU:0, one launch (start us, length us, event | category | flops | bytes accessed | tf_op | source)
XLA Modules:
  0.0 318.0 jit_solution(3767256040483934672)
XLA Ops:
  7.2 0.0 copy-start
  7.2 0.0 copy-start.4
  7.2 0.0 reduce-scatter.4.cloned.1.call-start
  7.2 0.9 copy-done
  8.2 4.9 %fusion.16 = f32[1408,512]{0,1:T(8,128)} fusion(f32[1408,64]{0,1:T(8,128)S(1)} %copy-done, f32[64,512]{1,0:T(8,128)} %param.7), kind=kOutput, calls=%fused_computation.32 | convolution fusion | flops 553648128 | bytes 3375104 | tf_op jit(solution)/shard_map/dot_general | solution.py:30
  13.1 0.0 reduce-scatter.4.cloned.1.call-update
  13.1 0.0 all-gather.3.cloned.1.call-start
  13.2 41.8 %reduce-scatter.4.cloned.1.call-done = f32[1408,64]{0,1:T(8,128)} async-done(((f32[1408,512]{0,1:T(8,128)}), f32[1408,64]{0,1:T(8,128)}) %reduce-scatter.4.cloned.1.call-update) | async-done | bytes 360464 | tf_op jit(solution)/shard_map/reduce_scatter | solution.py:33
  54.9 0.0 all-gather.3.cloned.1.call-update
  55.0 0.0 all-gather.5.cloned.1.call-start
  55.0 0.0 copy-done.4
  55.0 0.1 copy.13
  55.1 0.1 reduce-window.8
  55.2 0.1 add_reduce_fusion
  55.3 30.5 %all-gather.3.cloned.1.call-done = f32[5632,64]{0,1:T(8,128)} async-done(((f32[1408,64]{0,1:T(8,128)}), f32[5632,64]{0,1:T(8,128)}) %all-gather.3.cloned.1.call-update) | async-done | bytes 1441808 | tf_op jit(solution)/shard_map/all_gather | solution.py:34
  85.8 1.5 reshape.93
  87.3 0.6 fusion.7
  87.9 0.9 copy.26
  88.8 0.0 all-gather.5.cloned.1.call-update
  88.8 0.0 all-reduce.2.cloned.1.call-start
  88.9 18.8 %copy.14 = f32[1536,3072]{0,1:T(8,128)} copy(f32[1536,3072]{1,0:T(8,128)} %param.5) | data formatting | bytes 37748736 | tf_op args[0]
  107.7 18.7 %copy.15 = f32[1536,24,128]{2,0,1:T(8,128)} copy(f32[1536,24,128]{0,2,1:T(8,128)} %bitcast.34) | data formatting | bytes 37748736 | tf_op jit(solution)/shard_map/reshape | solution.py:50
  126.4 0.1 convert_reduce_fusion
  126.5 0.6 all-gather.5.cloned.1.call-done
  127.2 2.4 copy.17
  129.6 4.0 %fusion.2 = f32[12,128,512]{2,0,1:T(8,128)S(1)} fusion(f32[12,128,512]{2,1,0:T(8,128)S(1)} %bitcast.36, pred[]{:T(512)S(6)} %eq.41, s32[12]{0:T(128)S(1)} %get-tuple-element.6, s32[12]{0:T(128)S(1)} %get-tuple-element.7), kind=kOutput, calls=%fused_computation.5 | convolution fusion | flops 114032784 | bytes 6291553 | tf_op jit(solution)/shard_map/kp,pbw->kbw/dot_general | solution.py:16
  133.6 3.5 %copy.19 = f32[12,128,512]{2,1,0:T(8,128)} copy(f32[12,128,512]{2,0,1:T(8,128)S(1)} %fusion.2) | data formatting | bytes 6291456 | tf_op jit(solution)/shard_map/jit(_where)/select_n | solution.py:11
  137.1 0.0 all-reduce.2.cloned.1.call-update
  137.1 0.0 reduce-scatter.6.cloned.1.call-start
  137.2 12.3 %gather_fusion = f32[12,1536,128]{2,1,0:T(8,128)} fusion(f32[1536,24,128]{2,0,1:T(8,128)} %copy.15, s32[1024]{0:T(1024)S(1)} %pad_clamp_fusion), kind=kCustom, calls=%fused_computation | custom fusion | bytes 18874416 | tf_op jit(solution)/shard_map/jit(_take)/gather | solution.py:50
  149.5 9.8 %copy.16 = f32[1536,12,128]{0,2,1:T(8,128)} copy(f32[1536,12,128]{2,0,1:T(8,128)} %bitcast.35) | data formatting | bytes 18874368 | tf_op jit(solution)/shard_map/jit(_take)/gather | solution.py:50
  159.2 0.1 broadcast_bitcast_fusion
  159.3 0.0 copy-start.2
  159.3 4.6 %bitcast_select_fusion = f32[1536,1536]{0,1:T(8,128)S(1)} fusion(f32[1536,12,128]{0,2,1:T(8,128)} %copy.16, pred[1536]{0:T(1024)(128)(4,1)S(1)} %broadcast_bitcast_fusion), kind=kLoop, calls=%fused_computation.1 | loop fusion | flops 2359296 | bytes 18875904 | tf_op jit(solution)/shard_map/jit(_take)/select_n | solution.py:50
  164.0 0.1 copy-done.2
  164.0 17.1 %convolution_negate_fusion = f32[512,1536]{1,0:T(8,128)} fusion(f32[1536,512]{0,1:T(8,128)S(1)} %copy-done.2, f32[1536,1536]{0,1:T(8,128)S(1)} %bitcast_select_fusion), kind=kOutput, calls=%fused_computation.4 | convolution fusion | flops 14496301056 | bytes 15728640 | tf_op jit(solution)/shard_map/dot_general | solution.py:53
  181.1 0.0 copy-start.1
  181.1 0.0 copy-start.3
  181.1 0.0 reduce-scatter.6.cloned.1.call-update
  181.1 0.0 reduce-scatter.8.cloned.1.call-start
  181.2 42.4 %all-reduce.2.cloned.1.call-done = f32[1536,512]{1,0:T(8,128)} async-done(((f32[1536,512]{1,0:T(8,128)}), f32[1536,512]{1,0:T(8,128)}) %all-reduce.2.cloned.1.call-update) | async-done | bytes 3145744 | tf_op jit(solution)/shard_map/psum | solution.py:11
  223.6 47.3 %reduce-scatter.6.cloned.1.call-done = f32[128,1536]{1,0:T(8,128)} async-done(((f32[512,1536]{1,0:T(8,128)}), f32[128,1536]{1,0:T(8,128)}) %reduce-scatter.6.cloned.1.call-update) | async-done | bytes 786448 | tf_op jit(solution)/shard_map/reduce_scatter | solution.py:52
  270.9 7.8 %convolution_negate_fusion.1 = f32[512,128]{1,0:T(8,128)} fusion(f32[1536,512]{1,0:T(8,128)} %all-reduce.2.cloned.1.call-done, f32[128,1536]{1,0:T(8,128)} %reduce-scatter.6.cloned.1.call-done), kind=kOutput, calls=%fused_computation.6 | convolution fusion | flops 1208025088 | bytes 4194304 | tf_op jit(solution)/shard_map/dot_general | solution.py:69
  278.8 0.0 reduce-scatter.8.cloned.1.call-update
  278.8 31.0 %reduce-scatter.8.cloned.1.call-done = f32[64,128]{1,0:T(8,128)} async-done(((f32[512,128]{1,0:T(8,128)}), f32[64,128]{1,0:T(8,128)}) %reduce-scatter.8.cloned.1.call-update) | async-done | bytes 32784 | tf_op jit(solution)/shard_map/reduce_scatter | solution.py:76
  309.8 0.0 copy-done.3
  309.8 1.4 add.51
  311.1 0.0 copy-done.1
  (5 shorter events, 0.0 us)
Async XLA Ops:
  7.2 1.0 copy-start
  7.2 47.8 %copy-start.4 = (s32[44]{0:T(128)S(1)}, s32[44]{0:T(128)}, u32[]{:S(2)}) copy-start(s32[44]{0:T(128)} %param.9) | copy-start | bytes 532
  7.2 47.8 %reduce-scatter.4.cloned.1.call-start = ((), (), s32[]{:S(2)}) async-start(), calls=%async_computation.3 | async-start | bytes 3244032 | tf_op jit(solution)/shard_map/reduce_scatter | solution.py:33
  13.1 72.7 %all-gather.3.cloned.1.call-start = ((), (), s32[]{:S(2)}) async-start(), calls=%async_computation.4 | async-start | bytes 1802240 | tf_op jit(solution)/shard_map/all_gather | solution.py:34
  55.0 72.2 %all-gather.5.cloned.1.call-start = ((), (), s32[]{:S(2)}) async-start(), calls=%async_computation.5 | async-start | bytes 3538944 | tf_op jit(solution)/shard_map/all_gather | solution.py:49
  88.8 134.8 %all-reduce.2.cloned.1.call-start = ((), (), s32[]{:S(2)}) async-start(), calls=%async_computation.7 | async-start | bytes 6291456 | tf_op jit(solution)/shard_map/psum | solution.py:11
  137.1 133.8 %reduce-scatter.6.cloned.1.call-start = ((), (), s32[]{:S(2)}) async-start(), calls=%async_computation.6 | async-start | bytes 3932160 | tf_op jit(solution)/shard_map/reduce_scatter | solution.py:52
  159.3 4.7 %copy-start.2 = (f32[1536,512]{0,1:T(8,128)S(1)}, f32[1536,512]{0,1:T(8,128)}, u32[]{:S(2)}) copy-start(f32[1536,512]{0,1:T(8,128)} %all-gather.5.cloned.1.call-done) | copy-start | bytes 9437188
  181.1 130.0 %copy-start.1 = (f32[1408,64]{0,1:T(8,128)S(1)}, f32[1408,64]{0,1:T(8,128)}, u32[]{:S(2)}) copy-start(f32[1408,64]{0,1:T(8,128)} %param.6) | copy-start | bytes 1081348
  181.1 128.7 %copy-start.3 = (f32[64,128]{1,0:T(8,128)S(1)}, f32[64,128]{1,0:T(8,128)}, u32[]{:S(2)}) copy-start(f32[64,128]{1,0:T(8,128)} %param.8) | copy-start | bytes 98308
  181.1 128.6 %reduce-scatter.8.cloned.1.call-start = ((), (), s32[]{:S(2)}) async-start(), calls=%async_computation.8 | async-start | bytes 294912 | tf_op jit(solution)/shard_map/reduce_scatter | solution.py:76
Sparse Core Ops, SparseCore 0:
  13.2 41.6 reduce-scatter.3
  56.8 28.9 all-gather.2
  88.9 38.2 all-gather.4
  137.2 86.3 all-reduce.1
  227.0 43.8 reduce-scatter.5
  278.9 30.8 reduce-scatter.7
where the time goes:
time: 319 us; the launch traced here: 318 us
  waiting for transfers between devices  194 us (61%)
  local copies, waits for them, and re-layouts  68.9 us (22%)
  matrix products  34.5 us (11%)
  between operations  14.2 us (4%)
  other arithmetic  6.36 us (2%)
    reduce_scatter x1, waiting for transfers between devices, on_device(): lax.psum_scatter(-lax.dot_general(window, columns, (((0,), (1,)), ((), ()...  47.3 us
    psum x1, waiting for transfers between devices, broadcast(): return lax.psum(jnp.where(mine, value, jnp.zeros_like(value)), axis)  42.4 us
    reduce_scatter x1, waiting for transfers between devices, on_device(): lax.psum_scatter(partial_value, 'row', scatter_dimension=1, tiled=True)  41.8 us
    reduce_scatter x1, waiting for transfers between devices, on_device(): lax.psum_scatter(crossed, 'row', scatter_dimension=0, tiled=True)  31 us
    all_gather x1, waiting for transfers between devices, on_device(): all_rows = lax.all_gather(normal, 'col', axis=0, tiled=True)  30.5 us
    gather x2, local copies, waits for them, and re-layouts, on_device(): jnp.take(ancestor_inverse.reshape(rows_here, range_blocks, BLK), local_id...  22 us
    unnamed x12, local copies, waits for them, and re-layouts  20.7 us
    reshape x1, local copies, waits for them, and re-layouts, on_device(): ancestor_inverse.reshape(rows_here, range_blocks, BLK)  18.7 us
  transfers between devices with their start and end apart: 6, of which 6 were waited for; matrix products, arithmetic and copies ran while one was open for 26% of the time, Pallas kernels for 0%

commit v1 on v0

v1 whole, which is shorter than its diff:
```python
import functools

import jax
import jax.numpy as jnp
from jax import lax
from jax.experimental import pallas as pl
from jax.experimental.pallas import tpu as pltpu
from jax.sharding import PartitionSpec as P

BLK = 128
NT = (((1,), (1,)), ((), ()))


def select_kernel(per_shard, slots, ids_ref, live_ref, gathered_ref, out_ref):
    for slot in range(slots):
        block = ids_ref[slot]
        start = pl.multiple_of((block % per_shard) * BLK, BLK)
        value = gathered_ref[block // per_shard, :, pl.ds(start, BLK)]
        out_ref[:, slot * BLK : (slot + 1) * BLK] = jnp.where(live_ref[slot] > 0, value, 0.0)


def select(gathered, ids, live):
    slots = ids.shape[0]
    per_shard = gathered.shape[2] // BLK
    smem = pl.BlockSpec(memory_space=pltpu.SMEM)
    vmem = pl.BlockSpec(memory_space=pltpu.VMEM)
    return pl.pallas_call(
        functools.partial(select_kernel, per_shard, slots),
        out_shape=jax.ShapeDtypeStruct((gathered.shape[1], slots * BLK), jnp.float32),
        in_specs=[smem, smem, vmem],
        out_specs=vmem,
    )(ids, live, gathered)


def place_kernel(ids_ref, live_ref, value_ref, out_ref):
    out_ref[...] = jnp.where(live_ref[pl.program_id(0)] > 0, value_ref[...], 0.0)


def place(value, ids, live):
    width, blocks = value.shape[0], ids.shape[0]
    return pl.pallas_call(
        place_kernel,
        out_shape=jax.ShapeDtypeStruct((width, blocks * BLK), jnp.float32),
        grid_spec=pltpu.PrefetchScalarGridSpec(
            num_scalar_prefetch=2,
            grid=(blocks,),
            in_specs=[pl.BlockSpec((width, BLK), lambda b, ids, live: (0, ids[b]))],
            out_specs=pl.BlockSpec((width, BLK), lambda b, ids, live: (0, b)),
        ),
    )(ids, live, value)


def halves(value):
    high = value.astype(jnp.bfloat16)
    return high, (value - high.astype(jnp.float32)).astype(jnp.bfloat16)


def product_kernel(group, ids_ref, normal_ref, *refs):
    out_ref = refs[group]

    @pl.when(pl.program_id(1) == 0)
    def _():
        out_ref[...] = jnp.zeros_like(out_ref)

    n_high, n_low = halves(normal_ref[...])
    if group == 1:
        block = refs[0][...]
    else:
        block = jnp.concatenate([ref[...] for ref in refs[:group]], axis=1)
    a_high, a_low = halves(block)
    dot = functools.partial(
        lax.dot_general, dimension_numbers=NT, preferred_element_type=jnp.float32
    )
    out_ref[...] -= dot(n_high, a_high) + (dot(n_high, a_low) + dot(n_low, a_high))


def product(normal, ancestor, ids):
    width, slots = normal.shape[0], ids.shape[0]
    rows = ancestor.shape[0]
    group = 2 if slots % 2 == 0 else 1
    tile = 512 if rows % 512 == 0 else BLK

    def column(k):
        return pl.BlockSpec((tile, BLK), lambda i, j, ids: (i, ids[j * group + k]))

    return pl.pallas_call(
        functools.partial(product_kernel, group),
        out_shape=jax.ShapeDtypeStruct((width, rows), jnp.float32),
        grid_spec=pltpu.PrefetchScalarGridSpec(
            num_scalar_prefetch=1,
            grid=(rows // tile, slots // group),
            in_specs=[pl.BlockSpec((width, group * BLK), lambda i, j, ids: (0, j))]
            + [column(k) for k in range(group)],
            out_specs=pl.BlockSpec((width, tile), lambda i, j, ids: (0, i)),
        ),
        compiler_params=pltpu.CompilerParams(
            dimension_semantics=("arbitrary", "arbitrary"), vmem_limit_bytes=32 << 20
        ),
        cost_estimate=pl.CostEstimate(
            flops=6 * width * rows * slots * BLK,
            bytes_accessed=4 * (rows * slots * BLK + 2 * width * rows),
            transcendentals=0,
        ),
    )(ids, normal, *([ancestor] * group))


def on_device(ancestor_inverse, panel, unit_inverse, pivot_inverse, panel_blocks):
    high = lax.Precision.HIGH
    row_index = lax.axis_index("row")
    col_index = lax.axis_index("col")
    rows_here, cols_here = ancestor_inverse.shape
    width = unit_inverse.shape[1]
    block_total = panel_blocks.shape[0]
    range_blocks = cols_here // BLK
    row_blocks = rows_here // BLK
    first_block = col_index * range_blocks
    slot_count = range_blocks // 2

    gathered = lax.all_gather(panel.T, "col", axis=0, tiled=False)
    half = width // 2
    unit = [
        lax.all_gather(unit_inverse[:, k * half : (k + 1) * half], "row", axis=0, tiled=True)
        for k in range(2)
    ]

    in_range = (panel_blocks >= first_block) & (panel_blocks < first_block + range_blocks)
    order = jnp.arange(block_total, dtype=jnp.int32)
    upto = order[None, :] <= order[:, None]
    rank_of = jnp.sum((upto & in_range[None, :]).astype(jnp.int32), axis=1) - 1
    slot_ids = jnp.arange(slot_count, dtype=jnp.int32)
    selected = in_range[None, :] & (rank_of[None, :] == slot_ids[:, None])
    stored_ids = jnp.sum(jnp.where(selected, order[None, :], 0), axis=1)
    chosen_ids = jnp.sum(jnp.where(selected, panel_blocks[None, :], 0), axis=1)
    slot_live = jnp.sum(selected.astype(jnp.int32), axis=1)
    window_ids = jnp.where(slot_live > 0, chosen_ids, -1)
    local_ids = jnp.clip(chosen_ids - first_block, 0, range_blocks - 1)
    row_ids = row_index * row_blocks + jnp.arange(row_blocks, dtype=jnp.int32)
    match = window_ids[None, :] == row_ids[:, None]
    row_slot = jnp.sum(jnp.where(match, slot_ids[None, :], 0), axis=1)
    row_live = jnp.sum(match.astype(jnp.int32), axis=1)

    chosen = select(gathered, stored_ids, slot_live)
    window = lax.all_gather(chosen, "row", axis=0, tiled=True)
    normal = jnp.concatenate(
        [
            lax.dot_general(
                part,
                window,
                (((0,), (0,)), ((), ())),
                precision=high,
                preferred_element_type=jnp.float32,
            )
            for part in unit
        ],
        axis=0,
    )
    own_window = lax.psum(place(normal, row_slot, row_live), "col")
    inverse_tile = lax.psum_scatter(
        product(normal, ancestor_inverse, local_ids), "col", scatter_dimension=0, tiled=True
    )
    crossed = -lax.dot_general(
        own_window, inverse_tile, NT, precision=high, preferred_element_type=jnp.float32
    )
    parts = lax.all_to_all(
        crossed.reshape(width // pivot_inverse.shape[0], *pivot_inverse.shape), "row", 0, 0
    )
    diagonal_block = pivot_inverse + jnp.sum(parts, axis=0)
    return (inverse_tile, diagonal_block)


def solution(mesh):
    return jax.shard_map(
        on_device,
        mesh=mesh,
        in_specs=(P("row", "col"), P("col", "row"), P("row", None), P("row", "col"), P()),
        out_specs=(P("col", "row"), P("row", "col")),
        check_vma=False,
    )
```

time: 319 us -> 264 us (0.83)
  local copies, waits for them, and re-layouts: 68.9 us -> 4.4 us
  blocking collectives: 0 us -> 48.4 us
  waiting for transfers between devices: 194 us -> 154 us
  Pallas kernels: 0 us -> 27.4 us
  matrix products: 34.5 us -> 8.53 us
    reduce_scatter x3 -> x1, waiting for transfers between devices: 120 us -> 47.4 us  [on_device(): lax.psum_scatter(product(normal, ancestor_inverse, local_ids), 'col', sca...]
    all_gather x0 -> x2, blocking collectives: none -> 34.3 us  [on_device(): lax.all_gather(unit_inverse[:, k * half:(k + 1) * half], 'row', axis=0, t...]
    pallas_call x0 -> x3, Pallas kernels: none -> 27.4 us  [the longest x1 17.5 us: product(): pl.pallas_call(functools.partial(product_kernel, group), out_shape=jax.Sh...]
    dot_general x5 -> x3, matrix products: 34.5 us -> 8.53 us  [the longest x2 5.06 us: on_device(): lax.dot_general(part, window, (((0,), (0,)), ((), ())), precision=high, p...]
    psum x1, waiting for transfers between devices: 42.4 us -> 66.2 us  [on_device(): own_window = lax.psum(place(normal, row_slot, row_live), 'col')]
    gather x2 -> x0, local copies, waits for them, and re-layouts: 22 us -> none  [on_device(): jnp.take(ancestor_inverse.reshape(rows_here, range_blocks, BLK), local_id...]
    reshape x2 -> x0, local copies, waits for them, and re-layouts: 20.2 us -> none  [the longest x1 18.7 us: on_device(): ancestor_inverse.reshape(rows_here, range_blocks, BLK)]
    unnamed x12 -> x8, local copies, waits for them, and re-layouts: 20.7 us -> 3.52 us
  transfers between devices with their start and end apart: 6 -> 4, of which waited for: 6 -> 4; matrix products, arithmetic and copies ran while one was open for 26% -> 2% of each run, Pallas kernels for 0% -> 7%
where the time goes in v1:
time: 264 us; the launch traced here: 263 us
  waiting for transfers between devices  154 us (58%)
  blocking collectives  48.4 us (18%)
  Pallas kernels  27.4 us (10%)
  between operations  13.9 us (5%)
  matrix products  8.53 us (3%)
  other arithmetic  6.08 us (2%)
  local copies, waits for them, and re-layouts  4.4 us (2%)
    psum x1, waiting for transfers between devices, on_device(): own_window = lax.psum(place(normal, row_slot, row_live), 'col')  66.2 us
    reduce_scatter x1, waiting for transfers between devices, on_device(): lax.psum_scatter(product(normal, ancestor_inverse, local_ids), 'col', sca...  47.4 us
    all_gather x2, blocking collectives, on_device(): lax.all_gather(unit_inverse[:, k * half:(k + 1) * half], 'row', axis=0, t...  34.3 us
    all_gather x1, waiting for transfers between devices, on_device(): gathered = lax.all_gather(panel.T, 'col', axis=0, tiled=False)  32.3 us
    pallas_call x1, Pallas kernels, product(): pl.pallas_call(functools.partial(product_kernel, group), out_shape=jax.Sh...  17.5 us
    all_to_all x1, blocking collectives, on_device(): lax.all_to_all(crossed.reshape(width // pivot_inverse.shape[0], *pivot_in...  14.1 us
    pallas_call x1, Pallas kernels, place(): pl.pallas_call(place_kernel, out_shape=jax.ShapeDtypeStruct((width, block...  7.72 us
    all_gather x1, waiting for transfers between devices, on_device(): window = lax.all_gather(chosen, 'row', axis=0, tiled=True)  7.65 us
  transfers between devices with their start and end apart: 4, of which 4 were waited for; matrix products, arithmetic and copies ran while one was open for 2% of the time, Pallas kernels for 7%

profile of v1, /device:TPU:0, one launch (start us, length us, event | category | flops | bytes accessed | tf_op | source)
XLA Modules:
  0.0 263.0 jit_solution(8432185273866386710)
XLA Ops:
  7.2 0.0 all-gather.6.cloned.1.call-start
  7.2 0.7 all-gather.6.cloned.1.call-update
  7.9 0.0 all-gather.4.cloned.1.call-start
  8.0 0.7 compare_and_fusion
  8.6 0.1 convert_reduce_fusion
  8.7 1.3 convert_reduce_fusion.1
  10.1 32.3 %all-gather.6.cloned.1.call-done = f32[256,1408]{1,0:T(8,128)} async-done(((f32[64,1408]{1,0:T(8,128)}), f32[256,1408]{1,0:T(8,128)}) %all-gather.6.cloned.1.call-update) | async-done | bytes 1441808 | tf_op jit(solution)/shard_map/all_gather | solution.py:119
  42.3 2.2 shard_map.68
  44.5 0.0 all-gather.4.cloned.1.call-update
  44.6 0.0 all-reduce.2.cloned.1.call-start
  44.6 0.7 compare_select_fusion.1
  45.3 0.8 fusion.2
  46.1 0.9 fusion.4
  47.0 16.5 %all_gather.19 = f32[512,256]{1,0:T(8,128)S(1)} all-gather(f32[64,256]{1,0:T(8,128)S(1)} %get-tuple-element.8), channel_id=1, replica_groups=mesh['row'=8,'col'=4] {'row'}, dimensions={0}, use_global_device_ids=true | all-gather | bytes 589824 | tf_op jit(solution)/shard_map/all_gather | solution.py:122
  63.5 17.8 %all_gather.18 = f32[512,256]{1,0:T(8,128)S(1)} all-gather(f32[64,256]{1,0:T(8,128)S(1)} %get-tuple-element.7), channel_id=1, replica_groups=mesh['row'=8,'col'=4] {'row'}, dimensions={0}, use_global_device_ids=true | all-gather | bytes 589824 | tf_op jit(solution)/shard_map/all_gather | solution.py:122
  81.3 7.7 %all-gather.4.cloned.1.call-done = f32[512,1536]{1,0:T(8,128)} async-done(((f32[64,1536]{1,0:T(8,128)}), f32[512,1536]{1,0:T(8,128)}) %all-gather.4.cloned.1.call-update) | async-done | bytes 3145744 | tf_op jit(solution)/shard_map/all_gather | solution.py:143
  88.9 0.0 copy-start.2
  88.9 3.5 %convolution_bitcast_fusion = f32[256,1536]{1,0:T(8,128)S(1)} fusion(f32[512,1536]{1,0:T(8,128)} %all-gather.4.cloned.1.call-done, f32[512,256]{1,0:T(8,128)S(1)} %all_gather.19), kind=kOutput, calls=%fused_computation.1 | convolution fusion | flops 1207959552 | bytes 5242880 | tf_op jit(solution)/shard_map/dot_general | solution.py:146
  92.5 0.0 copy-done.2
  92.5 1.5 convolution_bitcast_fusion.1
  94.0 1.9 pad_maximum_fusion.normal_ref.value_ref
  95.9 7.7 %shard_map.70 = f32[512,1536]{1,0:T(8,128)} custom-call(s32[12]{0:T(128)} %get-tuple-element.3.ids_ref, s32[12]{0:T(128)} %get-tuple-element.2.live_ref, f32[512,1536]{1,0:T(8,128)} %pad_maximum_fusion.normal_ref.value_ref), custom_call_target="tpu_custom_call" | custom-call | tf_op jit(solution)/shard_map/pallas_call | solution.py:41
  103.6 0.0 copy-start
  103.6 0.0 all-reduce.2.cloned.1.call-update
  103.6 0.0 reduce-scatter.2.cloned.1.call-start
  103.7 1.8 copy-done
  105.5 17.5 %shard_map.69 = f32[512,1536]{1,0:T(8,128)S(1)} custom-call(s32[12]{0:T(128)S(1)} %get-tuple-element.10.ids_ref, f32[512,1536]{1,0:T(8,128)S(1)} %copy-done, f32[1536,3072]{1,0:T(8,128)} %refs_1_.1, f32[1536,3072]{1,0:T(8,128)} %refs_1_.1), custom_call_target="tpu_custom_call" | custom-call | flops 7247757312 | bytes 15728640 | tf_op jit(solution)/shard_map/pallas_call | solution.py:86
  123.0 0.0 copy-start.1
  123.0 1.7 copy-done.1
  124.7 0.0 reduce-scatter.2.cloned.1.call-update
  124.7 0.0 copy-start.3
  124.8 66.2 %all-reduce.2.cloned.1.call-done = f32[512,1536]{1,0:T(8,128)} async-done(((f32[512,1536]{1,0:T(8,128)}), f32[512,1536]{1,0:T(8,128)}) %all-reduce.2.cloned.1.call-update) | async-done | bytes 3145744 | tf_op jit(solution)/shard_map/psum | solution.py:157
  190.9 47.4 %reduce-scatter.2.cloned.1.call-done = f32[128,1536]{1,0:T(8,128)} async-done(((f32[512,1536]{1,0:T(8,128)}), f32[128,1536]{1,0:T(8,128)}) %reduce-scatter.2.cloned.1.call-update) | async-done | bytes 786448 | tf_op jit(solution)/shard_map/reduce_scatter | solution.py:158
  238.3 3.5 %convolution_negate_fusion = f32[512,128]{1,0:T(8,128)S(1)} fusion(f32[512,1536]{1,0:T(8,128)} %all-reduce.2.cloned.1.call-done, f32[128,1536]{1,0:T(8,128)} %reduce-scatter.2.cloned.1.call-done), kind=kOutput, calls=%fused_computation.3 | convolution fusion | flops 604045312 | bytes 4194304 | tf_op jit(solution)/shard_map/dot_general | solution.py:161
  241.8 14.1 %all_to_all.5 = f32[8,64,128]{2,1,0:T(8,128)S(1)} all-to-all(f32[8,64,128]{2,1,0:T(8,128)S(1)} %bitcast.14), channel_id=1, replica_groups=mesh['row'=8,'col'=4] {'row'}, dimensions={0} | all-to-all | bytes 524288 | tf_op jit(solution)/shard_map/all_to_all | solution.py:164
  255.9 0.0 copy-done.3
  255.9 0.6 add.28
  (3 shorter events, 0.0 us)
Async XLA Ops:
  7.2 35.2 %all-gather.6.cloned.1.call-start = ((), (), s32[]{:S(2)}) async-start(), calls=%async_computation.5 | async-start | bytes 1802240 | tf_op jit(solution)/shard_map/all_gather | solution.py:119
  7.9 81.0 %all-gather.4.cloned.1.call-start = ((), (), s32[]{:S(2)}) async-start(), calls=%async_computation.2 | async-start | bytes 3538944 | tf_op jit(solution)/shard_map/all_gather | solution.py:143
  44.6 146.4 %all-reduce.2.cloned.1.call-start = ((), (), s32[]{:S(2)}) async-start(), calls=%async_computation.4 | async-start | bytes 6291456 | tf_op jit(solution)/shard_map/psum | solution.py:157
  88.9 3.5 %copy-start.2 = (f32[512,1536]{1,0:T(8,128)S(1)}, f32[512,1536]{1,0:T(8,128)}, u32[]{:S(2)}) copy-start(f32[512,1536]{1,0:T(8,128)} %all-gather.4.cloned.1.call-done) | copy-start | bytes 9437188
  103.6 1.9 copy-start
  103.6 134.6 %reduce-scatter.2.cloned.1.call-start = ((), (), s32[]{:S(2)}) async-start(), calls=%async_computation.3 | async-start | bytes 3932160 | tf_op jit(solution)/shard_map/reduce_scatter | solution.py:158
  123.0 1.7 copy-start.1
  124.7 131.1 %copy-start.3 = (f32[64,128]{1,0:T(8,128)S(1)}, f32[64,128]{1,0:T(8,128)}, u32[]{:S(2)}) copy-start(f32[64,128]{1,0:T(8,128)} %param.8) | copy-start | bytes 98308
Sparse Core Ops, SparseCore 0:
  9.8 32.4 all-gather.5
  44.7 44.1 all-gather.3
  103.8 87.1 all-reduce.1
  194.3 43.8 reduce-scatter.1

commit v2 on v1

--- a/solution.py
+++ b/solution.py
@@ -11,43 +11,30 @@
 NT = (((1,), (1,)), ((), ()))
 
 
-def select_kernel(per_shard, slots, ids_ref, live_ref, gathered_ref, out_ref):
-    for slot in range(slots):
-        block = ids_ref[slot]
-        start = pl.multiple_of((block % per_shard) * BLK, BLK)
-        value = gathered_ref[block // per_shard, :, pl.ds(start, BLK)]
-        out_ref[:, slot * BLK : (slot + 1) * BLK] = jnp.where(live_ref[slot] > 0, value, 0.0)
+def select_kernel(per_shard, ids_ref, live_ref, gathered_ref, out_ref):
+    slots = out_ref.shape[2] // BLK
+    for target in range(out_ref.shape[0]):
+        for slot in range(slots):
+            at = target * slots + slot
+            block = ids_ref[at]
+            start = pl.multiple_of((block % per_shard) * BLK, BLK)
+            value = gathered_ref[block // per_shard, :, pl.ds(start, BLK)]
+            out_ref[target, :, slot * BLK : (slot + 1) * BLK] = jnp.where(
+                live_ref[at] > 0, value, 0.0
+            )
 
 
-def select(gathered, ids, live):
-    slots = ids.shape[0]
+def select(gathered, ids, live, targets):
+    slots = ids.shape[0] // targets
     per_shard = gathered.shape[2] // BLK
     smem = pl.BlockSpec(memory_space=pltpu.SMEM)
     vmem = pl.BlockSpec(memory_space=pltpu.VMEM)
     return pl.pallas_call(
-        functools.partial(select_kernel, per_shard, slots),
-        out_shape=jax.ShapeDtypeStruct((gathered.shape[1], slots * BLK), jnp.float32),
+        functools.partial(select_kernel, per_shard),
+        out_shape=jax.ShapeDtypeStruct((targets, gathered.shape[1], slots * BLK), jnp.float32),
         in_specs=[smem, smem, vmem],
         out_specs=vmem,
     )(ids, live, gathered)
-
-
-def place_kernel(ids_ref, live_ref, value_ref, out_ref):
-    out_ref[...] = jnp.where(live_ref[pl.program_id(0)] > 0, value_ref[...], 0.0)
-
-
-def place(value, ids, live):
-    width, blocks = value.shape[0], ids.shape[0]
-    return pl.pallas_call(
-        place_kernel,
-        out_shape=jax.ShapeDtypeStruct((width, blocks * BLK), jnp.float32),
-        grid_spec=pltpu.PrefetchScalarGridSpec(
-            num_scalar_prefetch=2,
-            grid=(blocks,),
-            in_specs=[pl.BlockSpec((width, BLK), lambda b, ids, live: (0, ids[b]))],
-            out_specs=pl.BlockSpec((width, BLK), lambda b, ids, live: (0, b)),
-        ),
-    )(ids, live, value)
 
 
 def halves(value):
@@ -106,7 +93,6 @@
 
 def on_device(ancestor_inverse, panel, unit_inverse, pivot_inverse, panel_blocks):
     high = lax.Precision.HIGH
-    row_index = lax.axis_index("row")
     col_index = lax.axis_index("col")
     rows_here, cols_here = ancestor_inverse.shape
     width = unit_inverse.shape[1]
@@ -132,29 +118,33 @@
     stored_ids = jnp.sum(jnp.where(selected, order[None, :], 0), axis=1)
     chosen_ids = jnp.sum(jnp.where(selected, panel_blocks[None, :], 0), axis=1)
     slot_live = jnp.sum(selected.astype(jnp.int32), axis=1)
-    window_ids = jnp.where(slot_live > 0, chosen_ids, -1)
     local_ids = jnp.clip(chosen_ids - first_block, 0, range_blocks - 1)
-    row_ids = row_index * row_blocks + jnp.arange(row_blocks, dtype=jnp.int32)
-    match = window_ids[None, :] == row_ids[:, None]
-    row_slot = jnp.sum(jnp.where(match, slot_ids[None, :], 0), axis=1)
-    row_live = jnp.sum(match.astype(jnp.int32), axis=1)
+    gathered, unit = lax.optimization_barrier((gathered, unit))
+    unit = jnp.concatenate(unit, axis=1)
+    rows, cols = lax.axis_size("row"), lax.axis_size("col")
+    chosen = select(gathered, stored_ids, slot_live, 1)[0]
+    window = lax.all_gather(chosen, "row", axis=0, tiled=True)
 
-    chosen = select(gathered, stored_ids, slot_live)
-    window = lax.all_gather(chosen, "row", axis=0, tiled=True)
-    normal = jnp.concatenate(
-        [
-            lax.dot_general(
-                part,
-                window,
-                (((0,), (0,)), ((), ())),
-                precision=high,
-                preferred_element_type=jnp.float32,
-            )
-            for part in unit
-        ],
-        axis=0,
-    )
-    own_window = lax.psum(place(normal, row_slot, row_live), "col")
+    match = panel_blocks[None, :] == jnp.arange(rows * row_blocks, dtype=jnp.int32)[:, None]
+    block_ids = jnp.sum(jnp.where(match, order[None, :], 0), axis=1)
+    block_live = jnp.sum(match.astype(jnp.int32), axis=1)
+    part = panel.shape[1] // cols
+    share = lax.dynamic_slice_in_dim(gathered, col_index * part, part, 1)
+    listed = lax.all_to_all(select(share, block_ids, block_live, rows), "row", 0, 0)
+    listed = lax.all_gather(listed, "col", axis=0, tiled=False).reshape(width, rows_here)
+    unit_mixed = unit.reshape(rows, cols, part, width).transpose(1, 0, 2, 3).reshape(width, width)
+
+    def normalise(factor, value):
+        return lax.dot_general(
+            factor,
+            value,
+            (((0,), (0,)), ((), ())),
+            precision=high,
+            preferred_element_type=jnp.float32,
+        )
+
+    normal = normalise(unit, window)
+    own_window = normalise(unit_mixed, listed)
     inverse_tile = lax.psum_scatter(
         product(normal, ancestor_inverse, local_ids), "col", scatter_dimension=0, tiled=True
     )

time: 264 us -> 218 us (0.83)
  waiting for transfers between devices: 154 us -> 68.8 us
  blocking collectives: 48.4 us -> 92 us
  Pallas kernels: 27.4 us -> 23.7 us
  matrix products: 8.53 us -> 12.2 us
  other arithmetic: 6.08 us -> 3.35 us
    psum x1 -> x0, waiting for transfers between devices: 66.2 us -> none  [on_device(): own_window = lax.psum(place(normal, row_slot, row_live), 'col')]
    all_to_all x0 -> x1, blocking collectives: none -> 46.6 us  [on_device(): lax.all_to_all(select(share, block_ids, block_live, rows), 'row', 0, 0)]
    all_gather x1, waiting for transfers between devices: 32.3 us -> 0.14 us  [on_device(): gathered = lax.all_gather(panel.T, 'col', axis=0, tiled=False)]
    all_gather x0 -> x1, waiting for transfers between devices: none -> 21 us  [on_device(): lax.all_gather(listed, 'col', axis=0, tiled=False).reshape(width, rows_here)]
    reduce_scatter x1, waiting for transfers between devices: 47.4 us -> 42.4 us  [on_device(): lax.psum_scatter(product(normal, ancestor_inverse, local_ids), 'col', sca...]
    pallas_call x2, Pallas kernels: 9.94 us -> 4.96 us  [select(): pl.pallas_call(functools.partial(select_kernel, per_shard), out_shape=jax...]
    dot_general x2, matrix products: 5.06 us -> 9.67 us  [normalise(): lax.dot_general(factor, value, (((0,), (0,)), ((), ())), precision=high,...]
    unnamed x8 -> x7, local copies, waits for them, and re-layouts: 3.52 us -> 0.07 us
  transfers between devices with their start and end apart: 4 -> 4, of which waited for: 4 -> 4; matrix products, arithmetic and copies ran while one was open for 2% -> 7% of each run, Pallas kernels for 7% -> 10%
where the time goes in v2:
time: 218 us; the launch traced here: 217 us
  blocking collectives  92 us (42%)
  waiting for transfers between devices  68.8 us (32%)
  Pallas kernels  23.7 us (11%)
  between operations  13.9 us (6%)
  matrix products  12.2 us (6%)
  other arithmetic  3.35 us (2%)
  local copies, waits for them, and re-layouts  2.74 us (1%)
    all_to_all x1, blocking collectives, on_device(): lax.all_to_all(select(share, block_ids, block_live, rows), 'row', 0, 0)  46.6 us
    reduce_scatter x1, waiting for transfers between devices, on_device(): lax.psum_scatter(product(normal, ancestor_inverse, local_ids), 'col', sca...  42.4 us
    all_gather x2, blocking collectives, on_device(): lax.all_gather(unit_inverse[:, k * half:(k + 1) * half], 'row', axis=0, t...  31.3 us
    all_gather x1, waiting for transfers between devices, on_device(): lax.all_gather(listed, 'col', axis=0, tiled=False).reshape(width, rows_here)  21 us
    pallas_call x1, Pallas kernels, product(): pl.pallas_call(functools.partial(product_kernel, group), out_shape=jax.Sh...  18.8 us
    all_to_all x1, blocking collectives, on_device(): lax.all_to_all(crossed.reshape(width // pivot_inverse.shape[0], *pivot_in...  14.1 us
    dot_general x2, matrix products, normalise(): lax.dot_general(factor, value, (((0,), (0,)), ((), ())), precision=high,...  9.67 us
    pallas_call x2, Pallas kernels, select(): pl.pallas_call(functools.partial(select_kernel, per_shard), out_shape=jax...  4.96 us
  transfers between devices with their start and end apart: 4, of which 4 were waited for; matrix products, arithmetic and copies ran while one was open for 7% of the time, Pallas kernels for 10%

profile of v2, /device:TPU:0, one launch (start us, length us, event | category | flops | bytes accessed | tf_op | source)
XLA Modules:
  0.0 216.8 jit_solution(14092006106985666948)
XLA Ops:
  7.2 0.0 copy-start.2
  7.2 0.0 all-gather.7.cloned.1.call-start
  7.2 0.7 all-gather.7.cloned.1.call-update
  7.9 0.0 all-gather.9.cloned.1.call-start
  8.0 0.7 compare_and_fusion
  8.6 0.1 convert_reduce_fusion.1
  8.7 1.3 convert_reduce_fusion.2
  10.0 0.9 fusion.6
  10.9 16.5 %all_gather.23 = f32[512,256]{1,0:T(8,128)S(1)} all-gather(f32[64,256]{1,0:T(8,128)S(1)} %get-tuple-element.14), channel_id=1, replica_groups=mesh['row'=8,'col'=4] {'row'}, dimensions={0}, use_global_device_ids=true | all-gather | bytes 589824 | tf_op jit(solution)/shard_map/all_gather | solution.py:108
  27.4 14.8 %all_gather.24 = f32[512,256]{1,0:T(8,128)S(1)} all-gather(f32[64,256]{1,0:T(8,128)S(1)} %get-tuple-element.13), channel_id=1, replica_groups=mesh['row'=8,'col'=4] {'row'}, dimensions={0}, use_global_device_ids=true | all-gather | bytes 589824 | tf_op jit(solution)/shard_map/all_gather | solution.py:108
  42.2 0.1 all-gather.7.cloned.1.call-done
  42.3 2.3 %shard_map.68 = f32[1,64,1536]{2,1,0:T(8,128)} custom-call(s32[12]{0:T(128)} %get-tuple-element.9.ids_ref, s32[12]{0:T(128)} %get-tuple-element.8.live_ref, f32[4,64,1408]{2,1,0:T(8,128)} %bitcast.20), custom_call_target="tpu_custom_call" | custom-call | tf_op jit(solution)/shard_map/pallas_call | solution.py:32
  44.6 0.0 all-gather.9.cloned.1.call-update
  44.6 0.0 all-gather.11.cloned.1.call-start
  44.7 0.0 copy-done.2
  44.7 0.6 convert_reduce_fusion
  45.3 1.7 constant_dynamic-slice_fusion.gathered_ref
  47.1 2.7 %shard_map.70 = f32[8,16,1536]{2,1,0:T(8,128)} custom-call(s32[96]{0:T(128)} %get-tuple-element.12.ids_ref, s32[96]{0:T(128)} %get-tuple-element.11.live_ref, f32[4,16,1408]{2,1,0:T(8,128)} %constant_dynamic-slice_fusion.gathered_ref), custom_call_target="tpu_custom_call" | custom-call | tf_op jit(solution)/shard_map/pallas_call | solution.py:32
  49.8 46.6 %all_to_all.10 = f32[8,16,1536]{2,1,0:T(8,128)} all-to-all(f32[8,16,1536]{2,1,0:T(8,128)} %shard_map.70), channel_id=1, replica_groups=mesh['row'=8,'col'=4] {'row'}, dimensions={0} | all-to-all | bytes 1572864 | tf_op jit(solution)/shard_map/all_to_all | solution.py:133
  96.3 0.0 all-gather.11.cloned.1.call-update
  96.3 0.0 reduce-scatter.2.cloned.1.call-start
  96.4 0.1 constant_dynamic-update-slice_fusion.1
  96.5 0.1 constant_dynamic-update-slice_fusion
  96.5 0.0 copy-start
  96.5 4.5 %all-gather.9.cloned.1.call-done = f32[1,512,1536]{2,1,0:T(8,128)} async-done(((f32[1,64,1536]{2,1,0:T(8,128)}), f32[1,512,1536]{2,1,0:T(8,128)}) %all-gather.9.cloned.1.call-update) | async-done | bytes 3145744 | tf_op jit(solution)/shard_map/all_gather | solution.py:126
  101.1 4.7 %fusion.normal_ref = f32[512,1536]{1,0:T(8,128)S(1)} fusion(f32[512,512]{1,0:T(8,128)S(1)} %constant_dynamic-update-slice_fusion, f32[1,512,1536]{2,1,0:T(8,128)} %all-gather.9.cloned.1.call-done), kind=kOutput, calls=%fused_computation.1 | convolution fusion | flops 2415919104 | bytes 7340032 | tf_op jit(solution)/shard_map/dot_general | solution.py:138
  105.8 0.0 copy-done
  105.8 18.8 %shard_map.69 = f32[512,1536]{1,0:T(8,128)} custom-call(s32[12]{0:T(128)S(1)} %subtract_clamp_fusion.ids_ref, f32[512,1536]{1,0:T(8,128)S(1)} %fusion.normal_ref, f32[1536,3072]{1,0:T(8,128)} %refs_1_.1, f32[1536,3072]{1,0:T(8,128)} %refs_1_.1), custom_call_target="tpu_custom_call" | custom-call | flops 7247757312 | bytes 15728640 | tf_op jit(solution)/shard_map/pallas_call | solution.py:73
  124.6 0.0 reduce-scatter.2.cloned.1.call-update
  124.6 21.0 %all-gather.11.cloned.1.call-done = f32[32,16,1536]{2,1,0:T(8,128)} async-done(((f32[8,16,1536]{2,1,0:T(8,128)}), f32[32,16,1536]{2,1,0:T(8,128)}) %all-gather.11.cloned.1.call-update) | async-done | bytes 3145744 | tf_op jit(solution)/shard_map/all_gather | solution.py:134
  145.6 5.0 %convolution_bitcast_fusion = f32[512,1536]{1,0:T(8,128)S(1)} fusion(f32[4,8,16,1536]{3,2,1,0:T(8,128)} %bitcast.24, f32[8,4,16,512]{3,2,1,0:T(8,128)} %bitcast.19), kind=kOutput, calls=%fused_computation | convolution fusion | flops 2415919104 | bytes 7340032 | tf_op jit(solution)/shard_map/dot_general | solution.py:138
  150.6 0.0 copy-start.1
  150.6 42.4 %reduce-scatter.2.cloned.1.call-done = f32[128,1536]{1,0:T(8,128)} async-done(((f32[512,1536]{1,0:T(8,128)}), f32[128,1536]{1,0:T(8,128)}) %reduce-scatter.2.cloned.1.call-update) | async-done | bytes 786448 | tf_op jit(solution)/shard_map/reduce_scatter | solution.py:148
  193.0 2.5 %convolution_negate_fusion = f32[512,128]{1,0:T(8,128)S(1)} fusion(f32[512,1536]{1,0:T(8,128)S(1)} %convolution_bitcast_fusion, f32[128,1536]{1,0:T(8,128)} %reduce-scatter.2.cloned.1.call-done), kind=kOutput, calls=%fused_computation.3 | convolution fusion | flops 604045312 | bytes 4194304 | tf_op jit(solution)/shard_map/dot_general | solution.py:151
  195.5 14.1 %all_to_all.11 = f32[8,64,128]{2,1,0:T(8,128)S(1)} all-to-all(f32[8,64,128]{2,1,0:T(8,128)S(1)} %bitcast.22), channel_id=1, replica_groups=mesh['row'=8,'col'=4] {'row'}, dimensions={0} | all-to-all | bytes 524288 | tf_op jit(solution)/shard_map/all_to_all | solution.py:154
  209.6 0.0 copy-done.1
  209.6 0.6 add.18
  (3 shorter events, 0.0 us)
Async XLA Ops:
  7.2 37.5 %copy-start.2 = (s32[44]{0:T(128)S(1)}, s32[44]{0:T(128)}, u32[]{:S(2)}) copy-start(s32[44]{0:T(128)} %param.9) | copy-start | bytes 532
  7.2 35.2 %all-gather.7.cloned.1.call-start = ((), (), s32[]{:S(2)}) async-start(), calls=%async_computation.4 | async-start | bytes 1802240 | tf_op jit(solution)/shard_map/all_gather | solution.py:105
  7.9 93.2 %all-gather.9.cloned.1.call-start = ((), (), s32[]{:S(2)}) async-start(), calls=%async_computation.5 | async-start | bytes 3538944 | tf_op jit(solution)/shard_map/all_gather | solution.py:126
  44.6 101.0 %all-gather.11.cloned.1.call-start = ((), (), s32[]{:S(2)}) async-start(), calls=%async_computation.6 | async-start | bytes 3932160 | tf_op jit(solution)/shard_map/all_gather | solution.py:134
  96.3 96.6 %reduce-scatter.2.cloned.1.call-start = ((), (), s32[]{:S(2)}) async-start(), calls=%async_computation.3 | async-start | bytes 3932160 | tf_op jit(solution)/shard_map/reduce_scatter | solution.py:148
  96.5 9.3 %copy-start = (f32[512,512]{1,0:T(8,128)}, f32[512,512]{1,0:T(8,128)S(1)}, u32[]{:S(2)}) copy-start(f32[512,512]{1,0:T(8,128)S(1)} %constant_dynamic-update-slice_fusion) | copy-start | bytes 3145732
  150.6 59.0 %copy-start.1 = (f32[64,128]{1,0:T(8,128)S(1)}, f32[64,128]{1,0:T(8,128)}, u32[]{:S(2)}) copy-start(f32[64,128]{1,0:T(8,128)} %param.8) | copy-start | bytes 98308
Sparse Core Ops, SparseCore 0:
  9.8 32.4 all-gather.6
  44.7 56.3 all-gather.8
  102.9 42.6 all-gather.10
  149.0 43.8 reduce-scatter.1
